TPU v7x, 32 devices: a whole 2x2x4 slice. The times are simulated.
32 devices in a mesh: ctx: 8 (over y, x, core), tensor: 4 (over z).
Axes of the slice: x: 2, y: 2, z: 4, core: 2. Of those that a mesh axis runs over, the one named last changes fastest.
Arguments:
- queries: bfloat16 [8192, 4096], P('ctx', 'tensor'), may hold values from -6 to 6
- keys: bfloat16 [8192, 4096], P('ctx', 'tensor'), may hold values from -6 to 6
- values: bfloat16 [8192, 4096], P('ctx', 'tensor'), may hold values from -6 to 6
- doc_ids: int32 [8192], P('ctx'), may hold values from 0 to 7, never falling along the last dimension, each value on 1 to 4096 neighbouring positions
- out_weight: bfloat16 [4096, 6144], P('tensor'), may hold values from -0.125 to 0.125
- grad_out: bfloat16 [8192, 6144], P('ctx', 'tensor'), may hold values from -6 to 6
Outputs:
- attended: bfloat16 [8192, 6144], P('ctx', 'tensor')
- grad_queries: bfloat16 [8192, 4096], P('ctx', 'tensor')
- grad_keys: bfloat16 [8192, 4096], P('ctx', 'tensor')
- grad_values: bfloat16 [8192, 4096], P('ctx', 'tensor')
- grad_weight: float32 [4096, 6144], P('tensor', 'ctx')
Inputs may be any that keep to these rules, and one draw needn't show every extreme that they name: `doc_ids`: never falling along the sequence; each document has 1 to 4096 positions, and one has exactly 4096.
All inputs are finite; a program needn't handle non-finite values.
Results may differ from a plain program's by a relative error of at most 0.015.
Values may be sent and summed in bfloat16 or wider, within the bound.
A program may use at most 192 MiB of HBM per device.

v0:
```python
import jax
import jax.numpy as jnp
from jax import lax
from jax.sharding import PartitionSpec as P

HEAD = 128
careful = lax.Precision.HIGH
epsilon = 1e-06


def prefix(value, axis, combine, identity, reverse):
    length, place = (lax.axis_size(axis), lax.axis_index(axis))
    everything = jax.tree.map(
        lambda part, kind: lax.all_gather(part.astype(kind), axis),
        value,
        (jnp.bfloat16, jnp.bfloat16),
    )
    start = jax.tree.map(
        lambda part, zero: jnp.broadcast_to(jnp.asarray(zero, part.dtype), part.shape),
        value,
        identity,
    )

    def turn(k, before):
        at = length - 1 - k if reverse else k
        reached = at > place if reverse else at < place
        new = combine(
            before, jax.tree.map(lambda part, own: part[at].astype(own.dtype), everything, value)
        )
        return jax.tree.map(lambda a, b: jnp.where(reached, a, b), new, before)

    return lax.fori_loop(0, length, turn, start)


def joined_state(earlier, later):
    earlier_doc, earlier_state = earlier
    later_doc, later_state = later
    vacant = later_doc < 0
    keeping = (earlier_doc == later_doc) | vacant
    doc_result = jnp.where(vacant, earlier_doc, later_doc)
    state_result = later_state + jnp.where(keeping, earlier_state, jnp.zeros_like(earlier_state))
    return (doc_result, state_result)


def carried(doc_cell, state, backward):
    identity = (jnp.full((1, 1, 1), -1.0, jnp.float32), jnp.zeros_like(state))
    if backward:
        doc_in, state_in = prefix((doc_cell, state), "ctx", joined_state, identity, True)
    else:
        doc_in, state_in = prefix((doc_cell, state), "ctx", joined_state, identity, False)
    return (doc_in.reshape(()), state_in)


def body(queries, keys, values, doc_ids, out_weight, grad_out):
    rows = queries.shape[0]
    head_size = HEAD
    heads_here = queries.shape[1] // head_size
    query_rows = queries.reshape(rows, heads_here, head_size)
    key_rows = keys.reshape(rows, heads_here, head_size)
    value_rows = values.reshape(rows, heads_here, head_size)
    doc_float = doc_ids.astype(jnp.float32)
    order = jnp.arange(rows)
    mask = ((order[:, None] >= order[None, :]) & (doc_float[:, None] == doc_float[None, :])).astype(
        jnp.float32
    )
    scores = (
        jnp.einsum("the,uhe->htu", query_rows, key_rows, preferred_element_type=jnp.float32)
        * mask[None]
    )
    local = jnp.einsum(
        "htu,uhf->thf", scores, value_rows, precision=careful, preferred_element_type=jnp.float32
    )
    tail_mask = (doc_float == doc_float[-1]).astype(jnp.bfloat16)[:, None, None]
    tail_state = jnp.einsum(
        "uhe,uhf->hef", key_rows * tail_mask, value_rows, preferred_element_type=jnp.float32
    )
    last_doc, state_in = carried(doc_float[-1].reshape(1, 1, 1), tail_state, False)
    joined = (doc_float == last_doc).astype(jnp.float32)[:, None, None]
    opened = local + joined * jnp.einsum(
        "the,hef->thf", query_rows, state_in, precision=careful, preferred_element_type=jnp.float32
    )
    inverse = lax.rsqrt(jnp.mean(opened * opened, axis=-1, keepdims=True) + epsilon)
    normed = opened * inverse
    normed_low = normed.reshape(rows, heads_here * head_size).astype(jnp.bfloat16)
    partial_out = jnp.dot(normed_low, out_weight, preferred_element_type=jnp.float32)
    attended = lax.psum_scatter(
        partial_out.astype(jnp.bfloat16), "tensor", scatter_dimension=1, tiled=True
    )
    grad_whole = lax.all_gather(grad_out, "tensor", axis=1, tiled=True)
    grad_normed = lax.dot_general(
        grad_whole, out_weight, (((1,), (1,)), ((), ())), preferred_element_type=jnp.float32
    )
    weight_term = lax.dot_general(
        normed_low, grad_whole, (((0,), (0,)), ((), ())), preferred_element_type=jnp.float32
    )
    grad_weight = lax.psum_scatter(
        weight_term.astype(jnp.bfloat16), "ctx", scatter_dimension=1, tiled=True
    ).astype(jnp.float32)
    grad_normed = grad_normed.reshape(rows, heads_here, head_size)
    grad_opened = inverse * (
        grad_normed - normed * jnp.mean(grad_normed * normed, axis=-1, keepdims=True)
    )
    head_mask = (doc_float == doc_float[0]).astype(jnp.bfloat16)[:, None, None]
    head_state = jnp.einsum(
        "the,thf->hef",
        query_rows * head_mask,
        grad_opened,
        precision=careful,
        preferred_element_type=jnp.float32,
    )
    first_doc, state_back = carried(doc_float[0].reshape(1, 1, 1), head_state, True)
    starts = (doc_float == first_doc).astype(jnp.float32)[:, None, None]
    grad_scores = (
        jnp.einsum(
            "thf,uhf->htu",
            grad_opened,
            value_rows,
            precision=careful,
            preferred_element_type=jnp.float32,
        )
        * mask[None]
    )
    grad_query = jnp.einsum(
        "htu,uhe->the", grad_scores, key_rows, precision=careful, preferred_element_type=jnp.float32
    ) + joined * jnp.einsum(
        "thf,hef->the", grad_opened, state_in, precision=careful, preferred_element_type=jnp.float32
    )
    grad_key = jnp.einsum(
        "htu,the->uhe",
        grad_scores,
        query_rows,
        precision=careful,
        preferred_element_type=jnp.float32,
    ) + starts * jnp.einsum(
        "uhf,hef->uhe",
        value_rows,
        state_back,
        precision=careful,
        preferred_element_type=jnp.float32,
    )
    grad_value = jnp.einsum(
        "htu,thf->uhf", scores, grad_opened, precision=careful, preferred_element_type=jnp.float32
    ) + starts * jnp.einsum(
        "uhe,hef->uhf", key_rows, state_back, precision=careful, preferred_element_type=jnp.float32
    )
    flat = heads_here * head_size
    return (
        attended,
        grad_query.reshape(rows, flat).astype(jnp.bfloat16),
        grad_key.reshape(rows, flat).astype(jnp.bfloat16),
        grad_value.reshape(rows, flat).astype(jnp.bfloat16),
        grad_weight,
    )


def solution(mesh):
    return jax.shard_map(
        body,
        mesh=mesh,
        in_specs=(
            P("ctx", "tensor"),
            P("ctx", "tensor"),
            P("ctx", "tensor"),
            P("ctx"),
            P("tensor", None),
            P("ctx", "tensor"),
        ),
        out_specs=(
            P("ctx", "tensor"),
            P("ctx", "tensor"),
            P("ctx", "tensor"),
            P("ctx", "tensor"),
            P("tensor", "ctx"),
        ),
        check_vma=False,
    )
```

profile of v0, /device:TPU:0, one launch (start us, length us, event | category | flops | bytes accessed | tf_op | source)
XLA Modules:
  0.0 642.6 jit_solution(15173689273183936138)
XLA Ops:
  8.6 3.6 copy.65
  12.2 4.1 copy.36
  17.6 3.1 fusion.46
  22.7 1.4 dynamic-update-slice
  24.1 1.4 dynamic-update-slice.1
  25.5 15.8 %all-reduce.2 = (bf16[8]{0:T(256)(128)(2,1)S(1)}, bf16[8]{0:T(256)(128)(2,1)}) all-reduce(bf16[8]{0:T(256)(128)(2,1)S(1)} %dynamic-update-slice, bf16[8]{0:T(256)(128)(2,1)S(1)} %dynamic-update-slice.1), channel_id=2, replica_groups=mesh['ctx'=8,'tensor'=4] {'ctx'}, use_global_device_ids=true, to_apply=%add | all-reduce | flops 16 | bytes 64
  41.3 4.0 copy.62
  45.3 2.8 fusion.17
  49.1 14.8 %fusion.32 = f32[8,1024,1024]{2,1,0:T(8,128)} fusion(bf16[1024,8,128]{0,2,1:T(8,128)(2,1)S(1)} %bitcast.128, bf16[1024,1024]{1,0:T(8,128)(2,1)S(1)} %copy-done.7), kind=kOutput, calls=%fused_computation.41 | convolution fusion | flops 2147483648 | bytes 37748736 | tf_op jit(solution)/shard_map/the,uhe->htu/dot_general | solution.py:67
  63.9 31.0 %while.34 = (s32[]{:T(128)}, f32[1,1,1]{2,1,0:T(1,128)}, f32[8,128,128]{2,1,0:T(8,128)S(1)}, s32[]{:T(128)}, bf16[8,1,1,1]{0,3,2,1:T(2,128)(2,1)S(1)}, /*index=5...) while((s32[]{:T(128)}, f32[1,1,1]{2,1,0:T(1,128)}, ...), condition=%wide.region_1.2_spmd.clone, body=%wide.region_0.1_spmd.clone.sunk | while | flops 655369 | bytes 1310887 | solution.py:32
  94.9 4.9 fusion.55
  99.8 21.0 %multiply_reduce_fusion.1 = (f32[1024,8]{0,1:T(8,128)S(1)}, f32[1024,8,128]{0,2,1:T(8,128)}) fusion(f32[8,128,1024]{2,1,0:T(8,128)} %fusion.55, f32[1024]{0:T(1024)S(1)} %compare_convert_fusion.2, f32[8,1024,1024]{2,1,0:T(8,128)} %fusion.32, f32[1024,1024]{1,0:T(8,128)} %fusion.17, bf16[1024,1024]{1,0:T(8,128)(2,1)S(1)} %copy-done), kind=kOutput, calls=%fused_computation.28 | convolution fusion | flops 6455025664 | bytes 48271360 | tf_op jit(solution)/shard_map/htu,uhf->thf/dot_general | solution.py:70
  120.8 150.5 %all-gather.8.cloned.1.call-done = bf16[1024,6144]{1,0:T(8,128)(2,1)} async-done(((bf16[1024,1536]{1,0:T(8,128)(2,1)}), bf16[1024,6144]{1,0:T(8,128)(2,1)}) %all-gather.8.cloned.1.call-update) | async-done | bytes 12582928 | tf_op jit(solution)/shard_map/all_gather | solution.py:89
  271.3 21.3 %multiply_reduce_fusion = (f32[1024,8]{0,1:T(8,128)S(1)}, f32[1024,1024]{0,1:T(8,128)S(1)}) fusion(f32[1024,8,128]{0,2,1:T(8,128)} %get-tuple-element.385, f32[1024,8]{0,1:T(8,128)S(1)} %add_rsqrt_fusion, bf16[1024,6144]{1,0:T(8,128)(2,1)} %all-gather.8.cloned.1.call-done, bf16[1024,6144]{1,0:T(8,128)(2,1)} %param.14), kind=kOutput, calls=%fused_computation.27 | convolution fusion | flops 12888039424 | bytes 33619968 | tf_op jit(solution)/shard_map/dot_general | solution.py:90
  292.7 3.0 subtract_multiply_fusion
  295.6 2.0 copy-done.3
  297.6 2.1 fusion.43
  299.7 20.9 %convolution_convert_fusion = bf16[1024,6144]{1,0:T(8,128)(2,1)} fusion(bf16[1024,1024]{0,1:T(8,128)(2,1)} %bitcast.136, bf16[1024,6144]{1,0:T(8,128)(2,1)} %all-gather.8.cloned.1.call-done), kind=kOutput, calls=%fused_computation.18 | convolution fusion | flops 12891193344 | bytes 27262976 | tf_op jit(solution)/shard_map/dot_general | solution.py:93
  320.7 22.6 %convolution_convert_fusion.1 = bf16[1024,6144]{1,0:T(8,128)(2,1)} fusion(bf16[1024,1024]{0,1:T(8,128)(2,1)} %bitcast.137, bf16[1024,6144]{1,0:T(8,128)(2,1)} %param.14), kind=kOutput, calls=%fused_computation.19 | convolution fusion | flops 12891193344 | bytes 27262976 | tf_op jit(solution)/shard_map/dot_general | solution.py:85
  343.4 7.2 %fusion.56 = f32[8,128,1024]{2,1,0:T(8,128)} fusion(f32[8,128,128]{2,1,0:T(8,128)S(1)} %get-tuple-element.271, f32[1024,8,128]{0,2,1:T(8,128)} %copy-done.3), kind=kOutput, calls=%fused_computation.67 | convolution fusion | flops 805306368 | bytes 8912896 | tf_op jit(solution)/shard_map/thf,hef->the/dot_general | solution.py:125
  350.6 18.5 %fusion.27 = f32[8,1024,1024]{2,1,0:T(8,128)} fusion(f32[1024,8,128]{0,2,1:T(8,128)} %copy-done.3, bf16[1024,1024]{1,0:T(8,128)(2,1)S(1)} %copy-done), kind=kOutput, calls=%fused_computation.36 | convolution fusion | flops 6442450944 | bytes 39845888 | tf_op jit(solution)/shard_map/thf,uhf->htu/dot_general | solution.py:114
  369.2 19.0 %fusion.15 = bf16[1024,8,128]{0,2,1:T(8,128)(2,1)} fusion(f32[8,128,1024]{2,1,0:T(8,128)} %fusion.56, bf16[1024,8,128]{0,2,1:T(8,128)(2,1)} %copy.36, f32[8,1024,1024]{2,1,0:T(8,128)} %fusion.27, f32[1024,1024]{1,0:T(8,128)S(1)} %copy-done.1, f32[1024]{0:T(1024)S(1)} %compare_convert_fusion.2), kind=kOutput, calls=%fused_computation.23 | convolution fusion | flops 6453985280 | bytes 46141440 | tf_op jit(solution)/shard_map/htu,uhe->the/dot_general | solution.py:123
  388.1 3.9 copy.52
  392.1 19.4 %fusion.6 = f32[8,128,1024]{2,1,0:T(8,128)} fusion(f32[1024,8,128]{0,2,1:T(8,128)} %copy-done.3, f32[8,1024,1024]{2,1,0:T(8,128)} %fusion.32, f32[1024,1024]{1,0:T(8,128)} %fusion.17), kind=kOutput, calls=%fused_computation.10 | convolution fusion | flops 6450839552 | bytes 46137344 | tf_op jit(solution)/shard_map/htu,thf->uhf/dot_general | solution.py:141
  411.4 31.1 %while.35 = (s32[]{:T(128)}, f32[1,1,1]{2,1,0:T(1,128)}, f32[8,128,128]{2,1,0:T(8,128)S(1)}, s32[]{:T(128)}, bf16[8,1,1,1]{0,3,2,1:T(2,128)(2,1)S(1)}, /*index=5...) while((s32[]{:T(128)}, f32[1,1,1]{2,1,0:T(1,128)}, ...), condition=%wide.region_6.7_spmd.clone, body=%wide.region_5.6_spmd.clone.sunk | while | flops 655373 | bytes 1310949 | solution.py:32
  442.5 5.7 add_convert_fusion
  448.2 3.9 copy.54
  452.2 1.3 fusion.25
  455.0 17.1 %fusion.14 = bf16[1024,8,128]{0,2,1:T(8,128)(2,1)} fusion(f32[8,128,1024]{2,1,0:T(8,128)S(1)} %fusion.25, bf16[1024,8,128]{0,2,1:T(8,128)(2,1)S(1)} %bitcast.130, f32[8,1024,1024]{2,1,0:T(8,128)} %fusion.27, f32[1024,1024]{1,0:T(8,128)S(1)} %copy-done.2, f32[1024]{0:T(1024)S(1)} %compare_convert_fusion), kind=kOutput, calls=%fused_computation.21 | convolution fusion | flops 6453985280 | bytes 46141440 | tf_op jit(solution)/shard_map/htu,the->uhe/dot_general | solution.py:128
  472.1 4.0 copy.53
  476.1 3.3 convert_element_type.139
  479.4 156.5 %reduce-scatter.3.cloned.1.call-done = bf16[1024,1536]{1,0:T(8,128)(2,1)} async-done(((bf16[1024,6144]{1,0:T(8,128)(2,1)}), bf16[1024,1536]{1,0:T(8,128)(2,1)}) %reduce-scatter.3.cloned.1.call-update) | async-done | bytes 3145744 | tf_op jit(solution)/shard_map/reduce_scatter | solution.py:86
  (85 shorter events, 37.7 us)
Async XLA Ops:
  7.2 10.4 %copy-start = (bf16[1024,1024]{1,0:T(8,128)(2,1)S(1)}, bf16[1024,1024]{1,0:T(8,128)(2,1)}, u32[]{:S(2)}) copy-start(bf16[1024,1024]{1,0:T(8,128)(2,1)} %param.12) | copy-start | bytes 6291460
  7.2 56.7 %all-gather.10.cloned.1.call-start = ((), (), s32[]{:S(2)}) async-start(), calls=%async_computation.5 | async-start | bytes 2359296 | tf_op jit(solution)/shard_map/all_gather | solution.py:14
  8.6 7.7 %copy-start.10 = (s32[1024]{0:T(1024)S(1)}, s32[1024]{0:T(1024)}, u32[]{:S(2)}) copy-start(s32[1024]{0:T(1024)} %param.13) | copy-start | bytes 12292
  17.6 3.9 copy-start.13
  20.7 250.5 %all-gather.8.cloned.1.call-start = ((), (), s32[]{:S(2)}) async-start(), calls=%async_computation.3 | async-start | bytes 15728640 | tf_op jit(solution)/shard_map/all_gather | solution.py:89
  21.5 389.9 %all-gather.12.cloned.1.call-start = ((), (), s32[]{:S(2)}) async-start(), calls=%async_computation.6 | async-start | bytes 2359296 | tf_op jit(solution)/shard_map/all_gather | solution.py:14
  45.3 2.8 copy-start.4
  45.3 3.8 copy-start.7
  271.3 21.3 %copy-start.8 = (f32[1024,8,128]{0,2,1:T(8,128)S(1)}, f32[1024,8,128]{0,2,1:T(8,128)}, u32[]{:S(2)}) copy-start(f32[1024,8,128]{0,2,1:T(8,128)} %get-tuple-element.385) | copy-start | bytes 12582916
  292.6 5.0 copy-start.5
  295.6 2.0 copy-start.3
  299.7 176.4 %reduce-scatter.5.cloned.1.call-start = ((), (), s32[]{:S(2)}) async-start(), calls=%async_computation.4 | async-start | bytes 14155776 | tf_op jit(solution)/shard_map/reduce_scatter | solution.py:96
  320.7 315.2 %reduce-scatter.3.cloned.1.call-start = ((), (), s32[]{:S(2)}) async-start(), calls=%async_computation.2 | async-start | bytes 15728640 | tf_op jit(solution)/shard_map/reduce_scatter | solution.py:86
  350.6 18.5 %copy-start.1 = (f32[1024,1024]{1,0:T(8,128)S(1)}, f32[1024,1024]{1,0:T(8,128)}, u32[]{:S(2)}) copy-start(f32[1024,1024]{1,0:T(8,128)} %fusion.17) | copy-start | bytes 12582916
  392.1 19.4 %copy-start.9 = (f32[8,128,128]{2,1,0:T(8,128)S(1)}, f32[8,128,128]{2,1,0:T(8,128)}, u32[]{:S(2)}) copy-start(f32[8,128,128]{2,1,0:T(8,128)} %custom-call.1) | copy-start | bytes 1572868
  392.1 19.4 %copy-start.12 = (bf16[8]{0:T(256)(128)(2,1)S(1)}, bf16[8]{0:T(256)(128)(2,1)}, u32[]{:S(2)}) copy-start(bf16[8]{0:T(256)(128)(2,1)} %get-tuple-element.375) | copy-start | bytes 52
  411.4 31.1 %copy-start.11 = (s32[1024]{0:T(1024)S(1)}, s32[1024]{0:T(1024)}, u32[]{:S(2)}) copy-start(s32[1024]{0:T(1024)} %param.13) | copy-start | bytes 12292
  452.2 2.2 copy-start.2
  452.2 2.9 copy-start.6
Sparse Core Ops, SparseCore 0:
  20.9 30.5 all-gather.9
  53.1 218.1 all-gather.7
  299.8 25.9 all-gather.11
  329.2 91.9 reduce-scatter.4
  423.9 211.8 reduce-scatter.2
where the time goes:
time: 652 us; the launch traced here: 643 us
  waiting for transfers between devices  308 us (47%)
  matrix products  199 us (31%)
  local copies, waits for them, and re-layouts  42.5 us (7%)
  loops' own time  31.9 us (5%)
  other arithmetic  31.5 us (5%)
  blocking collectives  15.8 us (2%)
  between operations  14.1 us (2%)
    reduce_scatter x1, waiting for transfers between devices, body(): lax.psum_scatter(partial_out.astype(jnp.bfloat16), 'tensor', scatter_dime...  156 us
    all_gather x1, waiting for transfers between devices, body(): grad_whole = lax.all_gather(grad_out, 'tensor', axis=1, tiled=True)  150 us
    another operation x2, loops' own time, prefix(): return lax.fori_loop(0, length, turn, start)  31.9 us
    unnamed x37, local copies, waits for them, and re-layouts  23.4 us
    dot_general x1, matrix products, body(): jnp.dot(normed_low, out_weight, preferred_element_type=jnp.float32)  22.6 us
    dot_general x1, matrix products, body(): lax.dot_general(grad_whole, out_weight, (((1,), (1,)), ((), ())), preferr...  21.3 us
    dot_general x1, matrix products, body(): jnp.einsum('htu,uhf->thf', scores, value_rows, precision=careful, preferr...  21 us
    dot_general x1, matrix products, body(): lax.dot_general(normed_low, grad_whole, (((0,), (0,)), ((), ())), preferr...  20.9 us
  transfers between devices with their start and end apart: 5, of which 2 were waited for; matrix products, arithmetic and copies ran while one was open for 36% of the time, Pallas kernels for 0%

commit v1 on v0

--- a/solution.py
+++ b/solution.py
@@ -86,7 +86,7 @@
     attended = lax.psum_scatter(
         partial_out.astype(jnp.bfloat16), "tensor", scatter_dimension=1, tiled=True
     )
-    grad_whole = lax.all_gather(grad_out, "tensor", axis=1, tiled=True)
+    grad_whole = jnp.concatenate(lax.all_gather(grad_out, "tensor"), axis=1)
     grad_normed = lax.dot_general(
         grad_whole, out_weight, (((1,), (1,)), ((), ())), preferred_element_type=jnp.float32
     )

time: 652 us -> 691 us (1.060)
  local copies, waits for them, and re-layouts: 42.5 us -> 96.3 us
  waiting for transfers between devices: 308 us -> 299 us
    reshape x0 -> x1, local copies, waits for them, and re-layouts: none -> 23.7 us  [body(): grad_whole = jnp.concatenate(lax.all_gather(grad_out, 'tensor'), axis=1)]
    all_gather x0 -> x1, local copies, waits for them, and re-layouts: none -> 17.3 us  [body(): grad_whole = jnp.concatenate(lax.all_gather(grad_out, 'tensor'), axis=1)]
    unnamed x37 -> x40, local copies, waits for them, and re-layouts: 23.4 us -> 36.5 us
    reduce_scatter x1, waiting for transfers between devices: 156 us -> 148 us  [body(): lax.psum_scatter(partial_out.astype(jnp.bfloat16), 'tensor', scatter_dime...]
  transfers between devices with their start and end apart: 5 -> 5, of which waited for: 2 -> 2; matrix products, arithmetic and copies ran while one was open for 36% -> 35% of each run, Pallas kernels for 0% -> 0%
where the time goes in v1:
time: 691 us; the launch traced here: 686 us
  waiting for transfers between devices  299 us (43%)
  matrix products  197 us (29%)
  local copies, waits for them, and re-layouts  96.3 us (14%)
  other arithmetic  31.5 us (5%)
  loops' own time  31.3 us (5%)
  blocking collectives  16.3 us (2%)
  between operations  14.1 us (2%)
    all_gather x1, waiting for transfers between devices, body(): grad_whole = jnp.concatenate(lax.all_gather(grad_out, 'tensor'), axis=1)  151 us
    reduce_scatter x1, waiting for transfers between devices, body(): lax.psum_scatter(partial_out.astype(jnp.bfloat16), 'tensor', scatter_dime...  148 us
    unnamed x40, local copies, waits for them, and re-layouts  36.5 us
    another operation x2, loops' own time, prefix(): return lax.fori_loop(0, length, turn, start)  31.3 us
    reshape x1, local copies, waits for them, and re-layouts, body(): grad_whole = jnp.concatenate(lax.all_gather(grad_out, 'tensor'), axis=1)  23.7 us
    dot_general x1, matrix products, body(): jnp.dot(normed_low, out_weight, preferred_element_type=jnp.float32)  22.3 us
    dot_general x1, matrix products, body(): lax.dot_general(grad_whole, out_weight, (((1,), (1,)), ((), ())), preferr...  21.5 us
    dot_general x1, matrix products, body(): jnp.einsum('htu,uhf->thf', scores, value_rows, precision=careful, preferr...  21.1 us
  transfers between devices with their start and end apart: 5, of which 2 were waited for; matrix products, arithmetic and copies ran while one was open for 35% of the time, Pallas kernels for 0%

profile of v1, /device:TPU:0, one launch (start us, length us, event | category | flops | bytes accessed | tf_op | source)
XLA Modules:
  0.0 686.0 jit_solution(15018766384384274481)
XLA Ops:
  8.6 3.6 copy.67
  12.2 4.1 copy.37
  17.6 3.1 fusion.46
  25.5 16.3 %all-reduce.2 = (bf16[8]{0:T(256)(128)(2,1)S(1)}, bf16[8]{0:T(256)(128)(2,1)}) all-reduce(bf16[8]{0:T(256)(128)(2,1)S(1)} %dynamic-update-slice, bf16[8]{0:T(256)(128)(2,1)S(1)} %dynamic-update-slice.1), channel_id=2, replica_groups=mesh['ctx'=8,'tensor'=4] {'ctx'}, use_global_device_ids=true, to_apply=%add | all-reduce | flops 16 | bytes 64
  41.9 4.0 copy.64
  45.8 2.8 fusion.17
  49.6 15.0 %fusion.32 = f32[8,1024,1024]{2,1,0:T(8,128)} fusion(bf16[1024,8,128]{0,2,1:T(8,128)(2,1)S(1)} %bitcast.133, bf16[1024,1024]{1,0:T(8,128)(2,1)S(1)} %copy-done.7), kind=kOutput, calls=%fused_computation.41 | convolution fusion | flops 2147483648 | bytes 37748736 | tf_op jit(solution)/shard_map/the,uhe->htu/dot_general | solution.py:67
  64.6 30.2 %while.34 = (s32[]{:T(128)}, f32[1,1,1]{2,1,0:T(1,128)}, f32[8,128,128]{2,1,0:T(8,128)S(1)}, s32[]{:T(128)}, bf16[8,1,1,1]{0,3,2,1:T(2,128)(2,1)S(1)}, /*index=5...) while((s32[]{:T(128)}, f32[1,1,1]{2,1,0:T(1,128)}, ...), condition=%wide.region_1.2_spmd.clone, body=%wide.region_0.1_spmd.clone.sunk | while | flops 655369 | bytes 1310887 | solution.py:32
  94.8 4.9 fusion.56
  99.7 21.1 %multiply_reduce_fusion.1 = (f32[1024,8]{0,1:T(8,128)S(1)}, f32[1024,8,128]{0,2,1:T(8,128)}) fusion(f32[8,128,1024]{2,1,0:T(8,128)} %fusion.56, f32[1024]{0:T(1024)S(1)} %compare_convert_fusion.2, f32[8,1024,1024]{2,1,0:T(8,128)} %fusion.32, f32[1024,1024]{1,0:T(8,128)} %fusion.17, bf16[1024,1024]{1,0:T(8,128)(2,1)S(1)} %copy-done), kind=kOutput, calls=%fused_computation.28 | convolution fusion | flops 6455025664 | bytes 48271360 | tf_op jit(solution)/shard_map/htu,uhf->thf/dot_general | solution.py:70
  120.7 150.6 %all-gather.11.cloned.1.call-done = bf16[4096,1536]{1,0:T(8,128)(2,1)} async-done(((bf16[1024,1536]{1,0:T(8,128)(2,1)}), bf16[4096,1536]{1,0:T(8,128)(2,1)}) %all-gather.11.cloned.1.call-update) | async-done | bytes 12582928 | tf_op jit(solution)/shard_map/all_gather | solution.py:89
  271.3 17.3 %copy.99 = bf16[4,1024,1536]{2,0,1:T(4,128)(2,1)} copy(bf16[4,1024,1536]{2,1,0:T(8,128)(2,1)} %bitcast.137) | data formatting | bytes 25165824 | tf_op jit(solution)/shard_map/all_gather | solution.py:89
  288.6 23.7 %reshape.150 = bf16[1024,6144,1]{1,0,2:T(8,128)(2,1)} reshape(bf16[1024,4,1536]{2,1,0:T(4,128)(2,1)} %bitcast.130) | data formatting | bytes 25165824 | tf_op jit(solution)/shard_map/reshape | solution.py:89
  312.3 21.5 %multiply_reduce_fusion = (f32[1024,8]{0,1:T(8,128)S(1)}, f32[1024,8,128]{0,2,1:T(8,128)S(1)}) fusion(f32[1024,8,128]{0,2,1:T(8,128)} %get-tuple-element.387, f32[1024,8]{0,1:T(8,128)S(1)} %add_rsqrt_fusion, bf16[1024,6144,1]{1,0,2:T(8,128)(2,1)} %reshape.150, bf16[8,128,6144]{2,1,0:T(8,128)(2,1)} %bitcast.147), kind=kOutput, calls=%fused_computation.27 | convolution fusion | flops 12888039424 | bytes 33619968 | tf_op jit(solution)/shard_map/dot_general | solution.py:90
  333.8 3.0 subtract_multiply_fusion
  336.8 2.0 copy-done.3
  338.7 2.1 fusion.43
  340.9 13.1 %copy.68 = bf16[128,8,4,1536]{3,1,2,0:T(8,128)(2,1)} copy(bf16[128,8,4,1536]{3,2,1,0:T(4,128)(2,1)} %bitcast.131) | data formatting | bytes 25165824
  354.0 20.3 %convolution_convert_fusion = bf16[1024,6144]{1,0:T(8,128)(2,1)} fusion(bf16[1024,1024]{0,1:T(8,128)(2,1)S(1)} %bitcast.144, bf16[1024,6144]{1,0:T(8,128)(2,1)} %bitcast.138), kind=kOutput, calls=%fused_computation.18 | convolution fusion | flops 12891193344 | bytes 27262976 | tf_op jit(solution)/shard_map/dot_general | solution.py:93
  374.4 22.3 %convolution_convert_fusion.1 = bf16[1024,6144]{1,0:T(8,128)(2,1)} fusion(bf16[1024,1024]{0,1:T(8,128)(2,1)} %bitcast.143, bf16[1024,6144]{1,0:T(8,128)(2,1)} %param.14), kind=kOutput, calls=%fused_computation.19 | convolution fusion | flops 12891193344 | bytes 27262976 | tf_op jit(solution)/shard_map/dot_general | solution.py:85
  396.8 6.1 fusion.57
  402.9 19.1 %fusion.27 = f32[8,1024,1024]{2,1,0:T(8,128)} fusion(f32[1024,8,128]{0,2,1:T(8,128)} %copy-done.3, bf16[1024,1024]{1,0:T(8,128)(2,1)S(1)} %copy-done), kind=kOutput, calls=%fused_computation.36 | convolution fusion | flops 6442450944 | bytes 39845888 | tf_op jit(solution)/shard_map/thf,uhf->htu/dot_general | solution.py:114
  421.9 18.4 %fusion.15 = bf16[1024,8,128]{0,2,1:T(8,128)(2,1)} fusion(f32[8,128,1024]{2,1,0:T(8,128)} %fusion.57, bf16[1024,8,128]{0,2,1:T(8,128)(2,1)} %copy.37, f32[8,1024,1024]{2,1,0:T(8,128)} %fusion.27, f32[1024,1024]{1,0:T(8,128)S(1)} %copy-done.1, f32[1024]{0:T(1024)S(1)} %compare_convert_fusion.2), kind=kOutput, calls=%fused_computation.23 | convolution fusion | flops 6453985280 | bytes 46141440 | tf_op jit(solution)/shard_map/htu,uhe->the/dot_general | solution.py:123
  440.4 3.9 copy.54
  444.3 18.7 %fusion.6 = f32[8,128,1024]{2,1,0:T(8,128)} fusion(f32[1024,8,128]{0,2,1:T(8,128)} %copy-done.3, f32[8,1024,1024]{2,1,0:T(8,128)} %fusion.32, f32[1024,1024]{1,0:T(8,128)} %fusion.17), kind=kOutput, calls=%fused_computation.10 | convolution fusion | flops 6450839552 | bytes 46137344 | tf_op jit(solution)/shard_map/htu,thf->uhf/dot_general | solution.py:141
  463.1 31.1 %while.35 = (s32[]{:T(128)}, f32[1,1,1]{2,1,0:T(1,128)}, f32[8,128,128]{2,1,0:T(8,128)S(1)}, s32[]{:T(128)}, bf16[8,1,1,1]{0,3,2,1:T(2,128)(2,1)S(1)}, /*index=5...) while((s32[]{:T(128)}, f32[1,1,1]{2,1,0:T(1,128)}, ...), condition=%wide.region_6.7_spmd.clone, body=%wide.region_5.6_spmd.clone.sunk | while | flops 655373 | bytes 1310949 | solution.py:32
  494.2 5.7 add_convert_fusion
  499.9 3.9 copy.56
  506.7 17.2 %fusion.14 = bf16[1024,8,128]{0,2,1:T(8,128)(2,1)} fusion(f32[8,128,1024]{2,1,0:T(8,128)S(1)} %fusion.25, bf16[1024,8,128]{0,2,1:T(8,128)(2,1)S(1)} %bitcast.135, f32[8,1024,1024]{2,1,0:T(8,128)} %fusion.27, f32[1024,1024]{1,0:T(8,128)S(1)} %copy-done.2, f32[1024]{0:T(1024)S(1)} %compare_convert_fusion), kind=kOutput, calls=%fused_computation.21 | convolution fusion | flops 6453985280 | bytes 46141440 | tf_op jit(solution)/shard_map/htu,the->uhe/dot_general | solution.py:128
  523.9 3.9 copy.55
  527.9 3.3 convert_element_type.140
  531.2 148.1 %reduce-scatter.3.cloned.1.call-done = bf16[1024,1536]{1,0:T(8,128)(2,1)} async-done(((bf16[1024,6144]{1,0:T(8,128)(2,1)}), bf16[1024,1536]{1,0:T(8,128)(2,1)}) %reduce-scatter.3.cloned.1.call-update) | async-done | bytes 3145744 | tf_op jit(solution)/shard_map/reduce_scatter | solution.py:86
  (90 shorter events, 41.6 us)
Async XLA Ops:
  7.2 10.4 %copy-start = (bf16[1024,1024]{1,0:T(8,128)(2,1)S(1)}, bf16[1024,1024]{1,0:T(8,128)(2,1)}, u32[]{:S(2)}) copy-start(bf16[1024,1024]{1,0:T(8,128)(2,1)} %param.12) | copy-start | bytes 6291460
  7.2 57.4 %all-gather.9.cloned.1.call-start = ((), (), s32[]{:S(2)}) async-start(), calls=%async_computation.4 | async-start | bytes 2359296 | tf_op jit(solution)/shard_map/all_gather | solution.py:14
  8.6 7.7 %copy-start.11 = (s32[1024]{0:T(1024)S(1)}, s32[1024]{0:T(1024)}, u32[]{:S(2)}) copy-start(s32[1024]{0:T(1024)} %param.13) | copy-start | bytes 12292
  17.6 3.9 copy-start.14
  20.7 250.6 %all-gather.11.cloned.1.call-start = ((), (), s32[]{:S(2)}) async-start(), calls=%async_computation.5 | async-start | bytes 15728640 | tf_op jit(solution)/shard_map/all_gather | solution.py:89
  21.5 441.5 %all-gather.13.cloned.1.call-start = ((), (), s32[]{:S(2)}) async-start(), calls=%async_computation.6 | async-start | bytes 2359296 | tf_op jit(solution)/shard_map/all_gather | solution.py:14
  45.8 2.8 copy-start.4
  45.8 3.8 copy-start.7
  312.3 21.5 %copy-start.8 = (f32[1024,8,128]{0,2,1:T(8,128)S(1)}, f32[1024,8,128]{0,2,1:T(8,128)}, u32[]{:S(2)}) copy-start(f32[1024,8,128]{0,2,1:T(8,128)} %get-tuple-element.387) | copy-start | bytes 12582916
  333.8 4.9 copy-start.5
  336.8 2.0 copy-start.3
  340.8 187.1 %reduce-scatter.5.cloned.1.call-start = ((), (), s32[]{:S(2)}) async-start(), calls=%async_computation.3 | async-start | bytes 14155776 | tf_op jit(solution)/shard_map/reduce_scatter | solution.py:96
  340.9 13.1 %copy-start.10 = (bf16[1024,8,128]{0,2,1:T(8,128)(2,1)S(1)}, bf16[1024,8,128]{0,2,1:T(8,128)(2,1)}, u32[]{:S(2)}) copy-start(bf16[1024,8,128]{0,2,1:T(8,128)(2,1)} %get-tuple-element.379) | copy-start | bytes 6291460
  374.3 304.9 %reduce-scatter.3.cloned.1.call-start = ((), (), s32[]{:S(2)}) async-start(), calls=%async_computation.2 | async-start | bytes 15728640 | tf_op jit(solution)/shard_map/reduce_scatter | solution.py:86
  402.9 19.1 %copy-start.1 = (f32[1024,1024]{1,0:T(8,128)S(1)}, f32[1024,1024]{1,0:T(8,128)}, u32[]{:S(2)}) copy-start(f32[1024,1024]{1,0:T(8,128)} %fusion.17) | copy-start | bytes 12582916
  444.3 18.8 %copy-start.9 = (f32[8,128,128]{2,1,0:T(8,128)S(1)}, f32[8,128,128]{2,1,0:T(8,128)}, u32[]{:S(2)}) copy-start(f32[8,128,128]{2,1,0:T(8,128)} %custom-call.1) | copy-start | bytes 1572868
  444.3 18.8 %copy-start.13 = (bf16[8]{0:T(256)(128)(2,1)S(1)}, bf16[8]{0:T(256)(128)(2,1)}, u32[]{:S(2)}) copy-start(bf16[8]{0:T(256)(128)(2,1)} %get-tuple-element.375) | copy-start | bytes 52
  463.0 31.2 %copy-start.12 = (s32[1024]{0:T(1024)S(1)}, s32[1024]{0:T(1024)}, u32[]{:S(2)}) copy-start(s32[1024]{0:T(1024)} %param.13) | copy-start | bytes 12292
  503.8 2.2 copy-start.2
  503.8 2.9 copy-start.6
Sparse Core Ops, SparseCore 0:
  20.9 30.6 all-gather.8
  53.1 218.1 all-gather.10
  341.0 25.9 all-gather.12
  374.5 90.0 reduce-scatter.4
  467.3 211.9 reduce-scatter.2
